TPU v7x, 32 devices: a whole 2x2x4 slice. The times are simulated.
32 devices in a mesh: gx: 2 (over x), gy: 4 (over z), gz: 4 (over y, core).
Axes of the slice: x: 2, y: 2, z: 4, core: 2. Of those that a mesh axis runs over, the one named last changes fastest.
Arguments:
- pair_list: int32 [1024, 2], P(('gx', 'gy', 'gz')), may hold values from 0 to 63, all different within a row; in each aligned block of 32 rows (0 to 31, 32 to 63, ...) at most 2 rows name the same one
- rank_bucket: int32 [1024], P(('gx', 'gy', 'gz')), may hold values from 0 to 2
- amplitudes: bfloat16 [1024, 36864], P(('gx', 'gy', 'gz')), may hold values from -0.4375 to 0.4375
- intersects: bfloat16 [1024, 36864], P(('gx', 'gy', 'gz')), may hold values from -0.4375 to 0.4375
- integrals: bfloat16 [1024, 36864], P(('gx', 'gy', 'gz')), may hold values from -6 to 6
- exchange_blocks: bfloat16 [64, 36864], P(('gx', 'gy')), may hold values from -0.4375 to 0.4375
Outputs:
- residuals: bfloat16 [1024, 36864], P(('gx', 'gy', 'gz'))
Inputs may be any that keep to these rules, and one draw needn't show every extreme that they name: `pair_list`: each row names two different occupied orbitals; within the rows of one device no orbital is named more than 2 times, a bound that some block reaches on some devices. `rank_bucket`: bucket b keeps the leading (b + 1) * 64 PNOs.
All inputs are finite; a program needn't handle non-finite values.
Results may differ from a plain program's by a relative error of at most 0.013.
Values may be sent and summed in bfloat16 or wider, within the bound.
A program may use at most 128 MiB of HBM per device.

v0:
```python
import jax
import jax.numpy as jnp
from jax import lax
from jax.sharding import PartitionSpec as P

RSTEP = 64
R = 192


def body(pair_list, rank_bucket, amplitudes, intersects, integrals, exchange_blocks):
    pair_rows = amplitudes.shape[0]
    rank_width = R
    owned_rows = exchange_blocks.shape[0]
    amplitudes = amplitudes.reshape(pair_rows, rank_width, rank_width)
    intersects = intersects.reshape(pair_rows, rank_width, rank_width)
    integrals = integrals.reshape(pair_rows, rank_width, rank_width)
    exchange_blocks = exchange_blocks.reshape(owned_rows, rank_width, rank_width)
    groups_x, groups_y = (lax.axis_size("gx"), lax.axis_size("gy"))
    group_total = groups_x * groups_y
    occupied = owned_rows * group_total
    row_index = lax.broadcasted_iota(jnp.int32, (rank_width, rank_width), 0)
    col_index = lax.broadcasted_iota(jnp.int32, (rank_width, rank_width), 1)
    pair_rank = (rank_bucket + 1) * RSTEP
    inside = (row_index[None] < pair_rank[:, None, None]) & (
        col_index[None] < pair_rank[:, None, None]
    )
    masked = jnp.where(inside, amplitudes, jnp.zeros_like(amplitudes))
    half_projected = jnp.einsum(
        "pab,pbc->pac", intersects, masked, preferred_element_type=jnp.float32
    ).astype(jnp.bfloat16)
    projected = jnp.einsum(
        "pab,pcb->pac", half_projected, intersects, preferred_element_type=jnp.float32
    ).astype(jnp.bfloat16)
    local_term = jnp.einsum("pab,pbc->pac", masked, integrals, preferred_element_type=jnp.float32)
    flat_projected = projected.reshape(pair_rows, rank_width * rank_width)
    end_counts = jnp.sum(
        (pair_list[None] == lax.broadcasted_iota(jnp.int32, (occupied, 1, 1), 0)).astype(jnp.int32),
        axis=2,
    ).astype(jnp.bfloat16)
    partial_sum = lax.psum_scatter(
        jnp.dot(end_counts, flat_projected, preferred_element_type=jnp.float32),
        ("gx", "gy"),
        scatter_dimension=0,
        tiled=True,
    ).reshape(owned_rows, rank_width, rank_width)
    domain = lax.psum(partial_sum, "gz")
    coupled = jnp.einsum(
        "oab,obc->oac",
        domain.astype(jnp.bfloat16),
        exchange_blocks,
        preferred_element_type=jnp.float32,
    ).astype(jnp.bfloat16)
    every_coupled, every_block = (
        lax.all_gather(coupled, ("gx", "gy"), axis=0, tiled=True),
        lax.all_gather(exchange_blocks, ("gx", "gy"), axis=0, tiled=True),
    )
    picked_blocks = every_block[pair_list]
    picked_coupled = every_coupled[pair_list]
    own_term = jnp.einsum(
        "pab,pebc->peac", projected, picked_blocks, preferred_element_type=jnp.float32
    ).astype(jnp.bfloat16)
    answers = (picked_coupled.astype(jnp.float32) - own_term.astype(jnp.float32)).astype(
        jnp.bfloat16
    )
    combined = (answers[:, 0].astype(jnp.float32) + answers[:, 1].astype(jnp.float32)).astype(
        jnp.bfloat16
    )
    half_back = jnp.einsum(
        "pba,pbc->pac", intersects, combined, preferred_element_type=jnp.float32
    ).astype(jnp.bfloat16)
    back_projected = jnp.einsum(
        "pab,pbc->pac", half_back, intersects, preferred_element_type=jnp.float32
    )
    residual_sum = integrals.astype(jnp.float32) + local_term + back_projected
    result = jnp.where(inside, residual_sum, jnp.zeros_like(residual_sum)).astype(jnp.bfloat16)
    return result.reshape(pair_rows, rank_width * rank_width)


def solution(mesh):
    placed = (
        P(("gx", "gy", "gz"), None),
        P(("gx", "gy", "gz")),
        P(("gx", "gy", "gz"), None),
        P(("gx", "gy", "gz"), None),
        P(("gx", "gy", "gz"), None),
        P(("gx", "gy"), None),
    )
    return jax.shard_map(
        body, mesh=mesh, in_specs=placed, out_specs=P(("gx", "gy", "gz"), None), check_vma=False
    )
```

profile of v0, /device:TPU:0, one launch (start us, length us, event | category | flops | bytes accessed | tf_op | source)
XLA Modules:
  0.0 454.9 jit_solution(4188154951140406437)
XLA Ops:
  6.5 0.0 reduce-scatter.2.cloned.1.call-start
  6.5 6.1 %reshape.28 = bf16[32,192,192]{2,1,0:T(8,128)(2,1)} reshape(bf16[32,36864]{1,0:T(8,128)(2,1)} %param.8) | data formatting | bytes 4718592 | tf_op jit(solution)/shard_map/reshape | solution.py:14
  12.7 0.0 copy-start.1
  12.7 5.0 %reshape.29 = bf16[32,192,192]{2,1,0:T(8,128)(2,1)S(1)} reshape(bf16[32,36864]{1,0:T(8,128)(2,1)} %param.9) | data formatting | bytes 4718592 | tf_op jit(solution)/shard_map/reshape | solution.py:15
  17.6 0.0 copy-done.1
  17.7 6.9 %fusion.19 = bf16[32,192,192]{2,1,0:T(8,128)(2,1)} fusion(bf16[32,192,192]{2,1,0:T(8,128)(2,1)S(1)} %reshape.29, bf16[32,192,192]{2,1,0:T(8,128)(2,1)} %reshape.28, s32[32]{0:T(128)S(1)} %add_multiply_fusion), kind=kOutput, calls=%fused_computation.20 | convolution fusion | flops 913047552 | bytes 7078016 | tf_op jit(solution)/shard_map/pab,pcb->pac/dot_general | solution.py:31
  24.5 0.0 copy-start
  24.5 6.2 %reshape.30 = bf16[32,36864]{1,0:T(8,128)(2,1)} reshape(bf16[32,192,192]{2,1,0:T(8,128)(2,1)} %fusion.19) | data formatting | bytes 4718592 | tf_op jit(solution)/shard_map/reshape | solution.py:35
  30.7 0.0 copy-done
  30.7 0.1 convert_reduce_fusion
  30.8 6.7 %fusion.26 = f32[64,36864]{1,0:T(8,128)} fusion(bf16[32,36864]{1,0:T(8,128)(2,1)} %reshape.30, s32[64,32]{0,1:T(8,128)S(1)} %convert_reduce_fusion), kind=kOutput, calls=%fused_computation.25 | convolution fusion | flops 150996992 | bytes 11804672 | tf_op jit(solution)/shard_map/dot_general | solution.py:41
  37.5 0.0 reduce-scatter.2.cloned.1.call-update
  37.5 0.0 all-gather.5.cloned.1.call-start
  37.5 2.9 reshape.32
  40.4 0.0 all-gather.5.cloned.1.call-update
  40.5 0.0 all-gather.3.cloned.1.call-start
  40.5 162.0 %reduce-scatter.2.cloned.1.call-done = f32[8,36864]{1,0:T(8,128)} async-done(((f32[64,36864]{1,0:T(8,128)}), f32[8,36864]{1,0:T(8,128)}) %reduce-scatter.2.cloned.1.call-update) | async-done | bytes 1179664 | tf_op jit(solution)/shard_map/reduce_scatter | solution.py:40
  202.5 3.1 reshape.31
  205.6 34.0 %all-reduce.1 = bf16[8,192,192]{2,1,0:T(8,128)(2,1)} all-reduce(f32[8,192,192]{2,1,0:T(8,128)} %reshape.31), channel_id=1, replica_groups=mesh['gx'=2,'gy'=4,'gz'=4] {'gz'}, use_global_device_ids=true, to_apply=%region_2.3 | all-reduce | flops 294912 | bytes 1769472 | tf_op jit(solution)/shard_map/psum | solution.py:46
  239.6 2.6 convolution_convert_fusion
  242.2 0.0 all-gather.3.cloned.1.call-update
  242.2 0.1 copy.24
  242.3 0.1 reshape.36
  242.4 6.3 %reshape.27 = bf16[32,192,192]{2,1,0:T(8,128)(2,1)} reshape(bf16[32,36864]{1,0:T(8,128)(2,1)} %param.10) | data formatting | bytes 4718592 | tf_op jit(solution)/shard_map/reshape | solution.py:16
  248.7 53.7 %all-gather.5.cloned.1.call-done = bf16[64,192,192]{2,1,0:T(8,128)(2,1)} async-done(((bf16[8,192,192]{2,1,0:T(8,128)(2,1)}), bf16[64,192,192]{2,1,0:T(8,128)(2,1)}) %all-gather.5.cloned.1.call-update) | async-done | bytes 4718608 | tf_op jit(solution)/shard_map/all_gather | solution.py:55
  302.4 6.3 %gather_fusion.1 = bf16[64,192,192]{2,1,0:T(8,128)(2,1)} fusion(bf16[64,192,192]{2,1,0:T(8,128)(2,1)} %all-gather.5.cloned.1.call-done, s32[1024]{0:T(1024)S(1)} %pad_clamp_fusion), kind=kCustom, calls=%fused_computation.1 | custom fusion | bytes 9437440 | tf_op jit(solution)/shard_map/gather | solution.py:57
  308.7 92.7 %all-gather.3.cloned.1.call-done = bf16[64,192,192]{2,1,0:T(8,128)(2,1)} async-done(((bf16[8,192,192]{2,1,0:T(8,128)(2,1)}), bf16[64,192,192]{2,1,0:T(8,128)(2,1)}) %all-gather.3.cloned.1.call-update) | async-done | bytes 4718608 | tf_op jit(solution)/shard_map/all_gather | solution.py:54
  401.4 6.4 %gather_fusion = bf16[64,192,192]{2,1,0:T(8,128)(2,1)} fusion(bf16[64,192,192]{2,1,0:T(8,128)(2,1)} %all-gather.3.cloned.1.call-done, s32[1024]{0:T(1024)S(1)} %pad_clamp_fusion), kind=kCustom, calls=%fused_computation | custom fusion | bytes 9437440 | tf_op jit(solution)/shard_map/gather | solution.py:58
  407.9 9.7 %copy.25 = f32[64,192,192]{1,2,0:T(8,128)} copy(bf16[64,192,192]{2,1,0:T(8,128)(2,1)} %gather_fusion) | data formatting | bytes 14155776 | tf_op jit(solution)/shard_map/convert_element_type | solution.py:62
  417.5 11.3 %fusion = bf16[32,2,192,192]{2,3,1,0:T(8,128)(2,1)} fusion(f32[32,2,192,192]{2,3,1,0:T(8,128)} %bitcast.27, bf16[32,2,192,192]{3,2,1,0:T(8,128)(2,1)} %bitcast.28, bf16[32,192,192]{2,1,0:T(8,128)(2,1)} %fusion.19), kind=kOutput, calls=%fused_computation.3 | convolution fusion | flops 915406848 | bytes 21233664 | tf_op jit(solution)/shard_map/pab,pebc->peac/dot_general | solution.py:59
  428.8 7.5 %fusion.9 = f32[32,192,192]{2,1,0:T(8,128)} fusion(bf16[32,192,192]{2,1,0:T(8,128)(2,1)S(1)} %reshape.29, bf16[32,2,192,192]{2,3,1,0:T(8,128)(2,1)} %fusion), kind=kOutput, calls=%fused_computation.15 | convolution fusion | flops 911867904 | bytes 15728640 | tf_op jit(solution)/shard_map/pab,pbc->pac/dot_general | solution.py:71
  436.3 7.9 %select_convert_fusion = bf16[32,192,192]{2,1,0:T(8,128)(2,1)S(1)} fusion(f32[32,192,192]{2,1,0:T(8,128)} %fusion.9, bf16[32,192,192]{2,1,0:T(8,128)(2,1)} %reshape.27, s32[32]{0:T(128)S(1)} %add_multiply_fusion, bf16[32,192,192]{2,1,0:T(8,128)(2,1)} %reshape.28), kind=kOutput, calls=%fused_computation.4 | convolution fusion | flops 467140608 | bytes 11796608 | tf_op jit(solution)/shard_map/pab,pbc->pac/dot_general | solution.py:34
  444.1 4.2 reshape.33
  (3 shorter events, 0.0 us)
Async XLA Ops:
  6.5 195.9 %reduce-scatter.2.cloned.1.call-start = ((), (), s32[]{:S(2)}) async-start(), calls=%async_computation.1 | async-start | bytes 10616832 | tf_op jit(solution)/shard_map/reduce_scatter | solution.py:40
  12.7 5.0 %copy-start.1 = (s32[32]{0:T(128)S(1)}, s32[32]{0:T(128)}, u32[]{:S(2)}) copy-start(s32[32]{0:T(128)} %param.7) | copy-start | bytes 388
  24.5 6.2 %copy-start = (s32[32,2]{0,1:T(2,128)S(1)}, s32[32,2]{0,1:T(2,128)}, u32[]{:S(2)}) copy-start(s32[32,2]{0,1:T(2,128)} %param.6) | copy-start | bytes 772
  37.5 264.9 %all-gather.5.cloned.1.call-start = ((), (), s32[]{:S(2)}) async-start(), calls=%async_computation.3 | async-start | bytes 7077888 | tf_op jit(solution)/shard_map/all_gather | solution.py:55
  40.5 361.0 %all-gather.3.cloned.1.call-start = ((), (), s32[]{:S(2)}) async-start(), calls=%async_computation.2 | async-start | bytes 7077888 | tf_op jit(solution)/shard_map/all_gather | solution.py:54
Sparse Core Ops, SparseCore 0:
  37.6 164.8 reduce-scatter.1
  204.6 97.7 all-gather.4
  304.5 96.8 all-gather.2
where the time goes:
time: 456 us; the launch traced here: 455 us
  waiting for transfers between devices  308 us (68%)
  local copies, waits for them, and re-layouts  56.5 us (12%)
  matrix products  42.8 us (9%)
  blocking collectives  34 us (7%)
  between operations  13.2 us (3%)
    reduce_scatter x1, waiting for transfers between devices, body(): lax.psum_scatter(jnp.dot(end_counts, flat_projected, preferred_element_ty...  162 us
    all_gather x1, waiting for transfers between devices, body(): lax.all_gather(coupled, ('gx', 'gy'), axis=0, tiled=True)  92.7 us
    all_gather x1, waiting for transfers between devices, body(): lax.all_gather(exchange_blocks, ('gx', 'gy'), axis=0, tiled=True)  53.7 us
    psum x1, blocking collectives, body(): domain = lax.psum(partial_sum, 'gz')  34 us
    dot_general x1, matrix products, body(): jnp.einsum('pab,pebc->peac', projected, picked_blocks, preferred_element_...  11.3 us
    convert_element_type x1, local copies, waits for them, and re-layouts, body(): picked_coupled.astype(jnp.float32) - own_term.astype(jnp.float32)  9.66 us
  transfers between devices with their start and end apart: 3, of which 3 were waited for; matrix products, arithmetic and copies ran while one was open for 5% of the time, Pallas kernels for 0%

commit v1 on v0

--- a/solution.py
+++ b/solution.py
@@ -43,7 +43,9 @@
         scatter_dimension=0,
         tiled=True,
     ).reshape(owned_rows, rank_width, rank_width)
-    domain = lax.psum(partial_sum, "gz")
+    domain = partial_sum
+    for hop in (1, 2):
+        domain = domain + lax.ppermute(domain, "gz", [(dev, dev ^ hop) for dev in range(4)])
     coupled = jnp.einsum(
         "oab,obc->oac",
         domain.astype(jnp.bfloat16),

time: 456 us -> 456 us (level)
  blocking collectives: 34 us -> 0 us
  waiting for transfers between devices: 308 us -> 341 us
    ppermute x0 -> x2, waiting for transfers between devices: none -> 38.6 us  [body(): lax.ppermute(domain, 'gz', [(dev, dev ^ hop) for dev in range(4)])]
    psum x1 -> x0, blocking collectives: 34 us -> none  [body(): domain = lax.psum(partial_sum, 'gz')]
    all_gather x1, waiting for transfers between devices: 53.7 us -> 47.4 us  [body(): lax.all_gather(exchange_blocks, ('gx', 'gy'), axis=0, tiled=True)]
  transfers between devices with their start and end apart: 3 -> 5, of which waited for: 3 -> 5; matrix products, arithmetic and copies ran while one was open for 5% -> 5% of each run, Pallas kernels for 0% -> 0%
where the time goes in v1:
time: 456 us; the launch traced here: 455 us
  waiting for transfers between devices  341 us (75%)
  local copies, waits for them, and re-layouts  56.2 us (12%)
  matrix products  41.6 us (9%)
  between operations  13.2 us (3%)
    reduce_scatter x1, waiting for transfers between devices, body(): lax.psum_scatter(jnp.dot(end_counts, flat_projected, preferred_element_ty...  162 us
    all_gather x1, waiting for transfers between devices, body(): lax.all_gather(coupled, ('gx', 'gy'), axis=0, tiled=True)  92.7 us
    all_gather x1, waiting for transfers between devices, body(): lax.all_gather(exchange_blocks, ('gx', 'gy'), axis=0, tiled=True)  47.4 us
    ppermute x2, waiting for transfers between devices, body(): lax.ppermute(domain, 'gz', [(dev, dev ^ hop) for dev in range(4)])  38.6 us
    dot_general x1, matrix products, body(): jnp.einsum('pab,pebc->peac', projected, picked_blocks, preferred_element_...  11.3 us
    convert_element_type x1, local copies, waits for them, and re-layouts, body(): picked_coupled.astype(jnp.float32) - own_term.astype(jnp.float32)  9.69 us
  transfers between devices with their start and end apart: 5, of which 5 were waited for; matrix products, arithmetic and copies ran while one was open for 5% of the time, Pallas kernels for 0%

profile of v1, /device:TPU:0, one launch (start us, length us, event | category | flops | bytes accessed | tf_op | source)
XLA Modules:
  0.0 455.0 jit_solution(6547689980813636764)
XLA Ops:
  6.5 0.0 reduce-scatter.2.cloned.1.call-start
  6.5 6.1 %reshape.28 = bf16[32,192,192]{2,1,0:T(8,128)(2,1)} reshape(bf16[32,36864]{1,0:T(8,128)(2,1)} %param.8) | data formatting | bytes 4718592 | tf_op jit(solution)/shard_map/reshape | solution.py:14
  12.7 0.0 copy-start.2
  12.7 5.0 %reshape.29 = bf16[32,192,192]{2,1,0:T(8,128)(2,1)S(1)} reshape(bf16[32,36864]{1,0:T(8,128)(2,1)} %param.9) | data formatting | bytes 4718592 | tf_op jit(solution)/shard_map/reshape | solution.py:15
  17.7 0.0 copy-done.2
  17.7 6.9 %fusion.19 = bf16[32,192,192]{2,1,0:T(8,128)(2,1)} fusion(bf16[32,192,192]{2,1,0:T(8,128)(2,1)S(1)} %reshape.29, bf16[32,192,192]{2,1,0:T(8,128)(2,1)} %reshape.28, s32[32]{0:T(128)S(1)} %add_multiply_fusion), kind=kOutput, calls=%fused_computation.20 | convolution fusion | flops 913047552 | bytes 7078016 | tf_op jit(solution)/shard_map/pab,pcb->pac/dot_general | solution.py:31
  24.6 0.0 copy-start.1
  24.6 6.2 %reshape.30 = bf16[32,36864]{1,0:T(8,128)(2,1)} reshape(bf16[32,192,192]{2,1,0:T(8,128)(2,1)} %fusion.19) | data formatting | bytes 4718592 | tf_op jit(solution)/shard_map/reshape | solution.py:35
  30.8 0.0 copy-done.1
  30.8 0.1 convert_reduce_fusion
  30.8 6.7 %fusion.25 = f32[64,36864]{1,0:T(8,128)} fusion(bf16[32,36864]{1,0:T(8,128)(2,1)} %reshape.30, s32[64,32]{0,1:T(8,128)S(1)} %convert_reduce_fusion), kind=kOutput, calls=%fused_computation.25 | convolution fusion | flops 150996992 | bytes 11804672 | tf_op jit(solution)/shard_map/dot_general | solution.py:41
  37.6 0.0 reduce-scatter.2.cloned.1.call-update
  37.6 0.0 all-gather.5.cloned.1.call-start
  37.6 2.9 reshape.32
  40.5 0.0 all-gather.5.cloned.1.call-update
  40.5 0.2 all-gather.3.cloned.1.call-start
  40.8 161.8 %reduce-scatter.2.cloned.1.call-done = f32[8,36864]{1,0:T(8,128)} async-done(((f32[64,36864]{1,0:T(8,128)}), f32[8,36864]{1,0:T(8,128)}) %reduce-scatter.2.cloned.1.call-update) | async-done | bytes 1179664 | tf_op jit(solution)/shard_map/reduce_scatter | solution.py:40
  202.6 3.1 reshape.31
  205.7 0.0 copy-start
  205.7 0.0 collective-permute-start
  205.7 3.6 collective-permute-done
  209.3 1.6 add.31
  210.9 1.5 collective-permute-start.1
  212.5 35.0 %collective-permute-done.1 = f32[8,192,192]{2,1,0:T(8,128)S(1)} collective-permute-done((f32[8,192,192]{2,1,0:T(8,128)S(1)}, f32[8,192,192]{2,1,0:T(8,128)S(1)}, u32[]{:S(2)}, u32[]{:S(2)}) %collective-permute-start.1) | collective-permute-done | bytes 1179680 | tf_op jit(solution)/shard_map/ppermute | solution.py:48
  247.4 0.0 copy-done
  247.4 1.3 convolution_convert_fusion
  248.7 0.0 all-gather.3.cloned.1.call-update
  248.7 0.1 copy.24
  248.8 0.1 reshape.36
  248.9 6.1 %reshape.27 = bf16[32,192,192]{2,1,0:T(8,128)(2,1)} reshape(bf16[32,36864]{1,0:T(8,128)(2,1)} %param.10) | data formatting | bytes 4718592 | tf_op jit(solution)/shard_map/reshape | solution.py:16
  255.1 47.4 %all-gather.5.cloned.1.call-done = bf16[64,192,192]{2,1,0:T(8,128)(2,1)} async-done(((bf16[8,192,192]{2,1,0:T(8,128)(2,1)}), bf16[64,192,192]{2,1,0:T(8,128)(2,1)}) %all-gather.5.cloned.1.call-update) | async-done | bytes 4718608 | tf_op jit(solution)/shard_map/all_gather | solution.py:57
  302.5 6.3 %gather_fusion.1 = bf16[64,192,192]{2,1,0:T(8,128)(2,1)} fusion(bf16[64,192,192]{2,1,0:T(8,128)(2,1)} %all-gather.5.cloned.1.call-done, s32[1024]{0:T(1024)S(1)} %pad_clamp_fusion), kind=kCustom, calls=%fused_computation.1 | custom fusion | bytes 9437440 | tf_op jit(solution)/shard_map/gather | solution.py:59
  308.8 92.7 %all-gather.3.cloned.1.call-done = bf16[64,192,192]{2,1,0:T(8,128)(2,1)} async-done(((bf16[8,192,192]{2,1,0:T(8,128)(2,1)}), bf16[64,192,192]{2,1,0:T(8,128)(2,1)}) %all-gather.3.cloned.1.call-update) | async-done | bytes 4718608 | tf_op jit(solution)/shard_map/all_gather | solution.py:56
  401.5 6.3 %gather_fusion = bf16[64,192,192]{2,1,0:T(8,128)(2,1)} fusion(bf16[64,192,192]{2,1,0:T(8,128)(2,1)} %all-gather.3.cloned.1.call-done, s32[1024]{0:T(1024)S(1)} %pad_clamp_fusion), kind=kCustom, calls=%fused_computation | custom fusion | bytes 9437440 | tf_op jit(solution)/shard_map/gather | solution.py:60
  407.8 9.7 %copy.25 = f32[64,192,192]{1,2,0:T(8,128)} copy(bf16[64,192,192]{2,1,0:T(8,128)(2,1)} %gather_fusion) | data formatting | bytes 14155776 | tf_op jit(solution)/shard_map/convert_element_type | solution.py:64
  417.5 11.3 %fusion = bf16[32,2,192,192]{2,3,1,0:T(8,128)(2,1)} fusion(f32[32,2,192,192]{2,3,1,0:T(8,128)} %bitcast.26, bf16[32,2,192,192]{3,2,1,0:T(8,128)(2,1)} %bitcast.27, bf16[32,192,192]{2,1,0:T(8,128)(2,1)} %fusion.19), kind=kOutput, calls=%fused_computation.3 | convolution fusion | flops 915406848 | bytes 21233664 | tf_op jit(solution)/shard_map/pab,pebc->peac/dot_general | solution.py:61
  428.8 7.5 %fusion.9 = f32[32,192,192]{2,1,0:T(8,128)} fusion(bf16[32,192,192]{2,1,0:T(8,128)(2,1)S(1)} %reshape.29, bf16[32,2,192,192]{2,3,1,0:T(8,128)(2,1)} %fusion), kind=kOutput, calls=%fused_computation.15 | convolution fusion | flops 911867904 | bytes 15728640 | tf_op jit(solution)/shard_map/pab,pbc->pac/dot_general | solution.py:73
  436.4 7.9 %select_convert_fusion = bf16[32,192,192]{2,1,0:T(8,128)(2,1)S(1)} fusion(f32[32,192,192]{2,1,0:T(8,128)} %fusion.9, bf16[32,192,192]{2,1,0:T(8,128)(2,1)} %reshape.27, s32[32]{0:T(128)S(1)} %add_multiply_fusion, bf16[32,192,192]{2,1,0:T(8,128)(2,1)} %reshape.28), kind=kOutput, calls=%fused_computation.4 | convolution fusion | flops 467140608 | bytes 11796608 | tf_op jit(solution)/shard_map/pab,pbc->pac/dot_general | solution.py:34
  444.2 4.2 reshape.33
  (3 shorter events, 0.0 us)
Async XLA Ops:
  6.5 196.0 %reduce-scatter.2.cloned.1.call-start = ((), (), s32[]{:S(2)}) async-start(), calls=%async_computation.1 | async-start | bytes 10616832 | tf_op jit(solution)/shard_map/reduce_scatter | solution.py:40
  12.7 5.0 %copy-start.2 = (s32[32]{0:T(128)S(1)}, s32[32]{0:T(128)}, u32[]{:S(2)}) copy-start(s32[32]{0:T(128)} %param.7) | copy-start | bytes 388
  24.6 6.2 %copy-start.1 = (s32[32,2]{0,1:T(2,128)S(1)}, s32[32,2]{0,1:T(2,128)}, u32[]{:S(2)}) copy-start(s32[32,2]{0,1:T(2,128)} %param.6) | copy-start | bytes 772
  37.6 264.9 %all-gather.5.cloned.1.call-start = ((), (), s32[]{:S(2)}) async-start(), calls=%async_computation.3 | async-start | bytes 7077888 | tf_op jit(solution)/shard_map/all_gather | solution.py:57
  40.5 361.0 %all-gather.3.cloned.1.call-start = ((), (), s32[]{:S(2)}) async-start(), calls=%async_computation.2 | async-start | bytes 7077888 | tf_op jit(solution)/shard_map/all_gather | solution.py:56
  205.7 41.7 %copy-start = (bf16[8,192,192]{2,1,0:T(8,128)(2,1)S(1)}, bf16[8,192,192]{2,1,0:T(8,128)(2,1)}, u32[]{:S(2)}) copy-start(bf16[8,192,192]{2,1,0:T(8,128)(2,1)} %reshape.32) | copy-start | bytes 1769476
  205.7 3.6 collective-permute-start
  210.9 36.5 %collective-permute-start.1 = (f32[8,192,192]{2,1,0:T(8,128)S(1)}, f32[8,192,192]{2,1,0:T(8,128)S(1)}, u32[]{:S(2)}, u32[]{:S(2)}) collective-permute-start(f32[8,192,192]{2,1,0:T(8,128)S(1)} %add.31), channel_id=1, source_target_pairs={{0,2},{1,3},{2,0},{3,1},{4,6},{5,7},{6,4},{7,5},{8,10},{9,11},{10,... | collective-permute-start | bytes 3538952 | tf_op jit(solution)/shard_map/ppermute | solution.py:48
Sparse Core Ops, SparseCore 0:
  37.7 164.8 reduce-scatter.1
  204.6 97.7 all-gather.4
  304.6 96.8 all-gather.2
